TPU v7x, 256 devices: a whole 4x4x8 slice. The times are simulated.
256 devices in a mesh: dp: 4 (over x), expert: 64 (over z, y, core).
Axes of the slice: x: 4, y: 4, z: 8, core: 2. Of those that a mesh axis runs over, the one named last changes fastest.
Arguments:
- tokens: bfloat16 [32768, 2048], P(('dp', 'expert')), may hold values from -6 to 6
- expert_ids: int32 [32768, 2], P(('dp', 'expert')), may hold values from 0 to 63, all different within a row; in each aligned block of 128 rows (0 to 127, 128 to 255, ...) at most 5 rows name the same one
- gate_units: int32 [32768, 2], P(('dp', 'expert')), may hold values from 64 to 1023
- capacity: int32 [64], replicated, may hold values from 512 to 1535
- w_gate: bfloat16 [64, 2048, 1408], P('expert', None, 'dp'), may hold values from -0.125 to 0.125
- w_up: bfloat16 [64, 2048, 1408], P('expert', None, 'dp'), may hold values from -0.125 to 0.125
- w_down: bfloat16 [64, 2048, 1408], P('expert', None, 'dp'), may hold values from -0.15625 to 0.15625
Outputs:
- mixed: bfloat16 [32768, 2048], P(('dp', 'expert'))
Inputs may be any that keep to these rules, and one draw needn't show every extreme that they name: `expert_ids`: each row names two different experts; of one device's 128 rows (aligned blocks) no expert is named more than 5 times.
All inputs are finite; a program needn't handle non-finite values.
Results may differ from a plain program's by a relative error of at most 0.0057.
Values may be sent and summed in bfloat16 or wider, within the bound.
A program may use at most 128 MiB of HBM per device.

v0:
```python
import functools

import jax
import jax.numpy as jnp
from jax import lax
from jax.experimental import pallas as pl
from jax.experimental.pallas import tpu as pltpu
from jax.sharding import Mesh
from jax.sharding import PartitionSpec as P

MESH = pl.DeviceIdType.MESH
AXES = ("dp", "expert_0", "expert_1", "expert_2")
EXPERT = ("expert_0", "expert_1", "expert_2")
BF16, F32, I32 = jnp.bfloat16, jnp.float32, jnp.int32
LANES = 128
ROW_TILE = 16


def offset_groups(nz, ny):
    if (nz, ny) != (8, 4):
        first = [(dz, dy) for dz in (0, 1) for dy in range(ny)]
        return [first] + [
            [(dz, dy) for dz in (k + 1, -k) for dy in range(ny)] for k in reversed(range(1, nz // 2))
        ]
    return [
        [(0, 0), (0, 1), (0, 2), (0, 3), (1, 0), (-1, 0), (1, 3), (-1, 3)],
        [(-2, 2), (-2, 3), (2, 2), (2, 3), (3, 0), (-3, 0), (3, 1), (-3, 1)],
        [(4, 0), (4, 1), (3, 2), (3, 3), (-3, 2), (-3, 3), (4, 2), (4, 3)],
        [(1, 1), (-1, 1), (1, 2), (-1, 2), (2, 0), (-2, 0), (2, 1), (-2, 1)],
    ]


def log2(n):
    assert n & (n - 1) == 0
    return n.bit_length() - 1


def kernel(
    shape, most,
    tokens_h, ids_h, units_h, cap_h, wg_h, wu_h, wd_h, out,
    tokens, ids, units, cap, wg, wu, wd, perm, rows2d, out3, recv3, ret3, back3, a2d, hid, own, pf, part, rs1, rs2,
    sel, whi, wlo, acc, cnt_mine, cnt_all, tot_mine, tot_all,
    fx, fr, fs, fb, f1, f2, fsum, relayed,
    near, w_sem, a2a_send, a2a_recv, ag_send, ag_recv, rs_send, rs_recv, back_send, back_recv, cnt_send, cnt_recv, tot_send, tot_recv,
    fx_send, fx_recv, fb_send, fb_recv, relay_send, relay_recv,
):
    nx, nz, ny, nc = shape
    x, z, y, c = (lax.axis_index(a) for a in AXES)
    right, left, opp = lax.rem(x + 1, nx), lax.rem(x + nx - 1, nx), lax.rem(x + 2, nx)
    plane = nz * ny * nc
    per_z = ny * nc
    groups = offset_groups(nz, ny)
    per_group = len(groups[0]) * nc
    far = [g for g, group in enumerate(groups) if group[0][0] == nz // 2 > 1]
    far_offsets = min(2, ny)
    gr = per_group * most
    blocks = gr // ROW_TILE
    t_rows, width = tokens.shape
    half = width // 2
    lo, hi = pl.ds(0, half), pl.ds(half, half)

    def at_x(new_x):
        return (new_x, z, y, c)

    def relative(sign, dz, dy, dc):
        return (
            x,
            lax.rem(z + sign * dz + 2 * nz, nz),
            lax.rem(y + sign * dy + ny, ny),
            lax.rem(c + sign * dc + nc, nc),
        )

    def split(i):
        return i // per_z, lax.rem(i // nc, ny), lax.rem(i, nc)

    barrier = pltpu.get_barrier_semaphore()
    nearby = min(3, nz) * per_z

    def greet(i, carry):
        dz, dy, dc = split(i)
        dz = jnp.where(dz == 2, -1, dz)
        pl.semaphore_signal(barrier, inc=1, device_id=relative(1, dz, dy, dc), device_id_type=MESH)
        return carry

    for new_x in (right, left, opp):
        pl.semaphore_signal(barrier, inc=1, device_id=at_x(new_x), device_id_type=MESH)
    lax.fori_loop(1, nearby, greet, 0)

    small = [
        pltpu.make_async_copy(src, dst, w_sem.at[i])
        for i, (src, dst) in enumerate(((ids_h, ids), (tokens_h, tokens), (units_h, units), (cap_h, cap)))
    ]
    loads = [
        pltpu.make_async_copy(src.at[0], dst, w_sem.at[4 + i])
        for i, (src, dst) in enumerate(((wg_h, wg), (wu_h, wu), (wd_h, wd)))
    ]
    for load in small + loads:
        load.start()

    def near_ready():
        pl.semaphore_wait(barrier, nearby - 1 + nx - 1)

    def tell(step):
        for dz in (1, -1):
            pl.semaphore_signal(near.at[step], inc=1, device_id=relative(1, dz, 0, 0), device_id_type=MESH)

    def told(step):
        pl.semaphore_wait(near.at[step], 2)

    i_row = lax.broadcasted_iota(I32, (256, 256), 0)
    i_col = lax.broadcasted_iota(I32, (256, 256), 1)
    swapped = (i_row & 15) * 16 + lax.shift_right_logical(i_row, 4)
    perm[...] = (i_col == swapped).astype(BF16)
    small[0].wait()

    n_experts = cap.shape[1]
    expert = lax.broadcasted_iota(I32, (n_experts, t_rows), 0)
    id0, id1 = ids[0:1, :], ids[1:2, :]
    oh0, oh1 = (expert == id0).astype(F32), (expert == id1).astype(F32)
    named = (oh0 + oh1).astype(BF16)
    counts = lax.dot_general(
        jnp.ones((8, t_rows), BF16), named, (((1,), (1,)), ((), ())), preferred_element_type=F32
    )[0:1, :]
    cnt_mine[:, 0:n_experts] = counts
    cnt_all[0, :, 0:n_experts] = counts
    earlier = (
        lax.broadcasted_iota(I32, (t_rows, t_rows), 0) < lax.broadcasted_iota(I32, (t_rows, t_rows), 1)
    ).astype(BF16)
    before = jnp.dot(named, earlier, preferred_element_type=F32)
    rank0 = jnp.sum(before * oh0, axis=0, keepdims=True)
    rank1 = jnp.sum(before * oh1, axis=0, keepdims=True)

    def slot_of(expert, rank):
        ez = lax.shift_right_logical(expert, log2(per_z))
        ey = lax.shift_right_logical(expert, log2(nc)) & (ny - 1)
        ec = expert & (nc - 1)
        dz = (ez - z + nz) & (nz - 1)
        dy = (ey - y + ny) & (ny - 1)
        dc = (ec - c + nc) & (nc - 1)
        key, place = dz * ny + dy, jnp.zeros_like(dz)
        for i, (z_off, y_off) in enumerate(pair for group in groups for pair in group):
            place = jnp.where(key == (z_off % nz) * ny + y_off, i, place)
        return (place * nc + dc) * most + rank.astype(I32)

    pos0, pos1 = slot_of(id0, rank0), slot_of(id1, rank1)
    small[1].wait()

    def to_tiles(src, dst3, r0):
        for b in range(blocks):
            block = src[ROW_TILE * b : ROW_TILE * (b + 1), :]
            stacked = jnp.concatenate(
                [block[:, LANES * s : LANES * (s + 1)] for s in range(width // LANES)], axis=0
            )
            turned = jnp.dot(perm[...], stacked, preferred_element_type=F32).astype(BF16)
            r = r0 + ROW_TILE * b
            dst3[r : r + ROW_TILE] = turned.reshape(ROW_TILE, ROW_TILE, LANES)

    def from_tiles(block_of, dst):
        for b in range(blocks):
            stacked = block_of(ROW_TILE * b).reshape(ROW_TILE * ROW_TILE, LANES)
            turned = jnp.dot(perm[...], stacked, preferred_element_type=F32).astype(BF16)
            for s in range(width // LANES):
                dst[ROW_TILE * b : ROW_TILE * (b + 1), LANES * s : LANES * (s + 1)] = turned[
                    ROW_TILE * s : ROW_TILE * (s + 1), :
                ]

    def block_in(src3, r0):
        return lambda r: src3[r0 + r : r0 + r + ROW_TILE]

    def exchange(src, dst, g, sign, send_sem, recv_sem):
        base = g * per_group if g else 0
        for i, (dz, dy) in enumerate(groups[g]):
            for dc in range(nc):
                rows = pl.ds((base + i * nc + dc) * most, most)
                rows = rows if g else (slice(None), rows)
                if dz == dy == dc == 0:
                    assert i == 0
                    continue
                target, arrival, z_off = dst.at[rows], recv_sem.at[g], sign * dz
                if g in far and i < far_offsets:
                    way = 0 if sign == 1 else 1
                    target = relayed.at[way, pl.ds((i * nc + dc) * most, most)]
                    arrival, z_off = relay_recv.at[way], -(nz // 4)
                pltpu.make_async_remote_copy(
                    src_ref=src.at[rows],
                    dst_ref=target,
                    send_sem=send_sem.at[g],
                    recv_sem=arrival,
                    device_id=relative(1, z_off, sign * dy, sign * dc),
                    device_id_type=MESH,
                ).start()
        if g == 0:
            dst[:, 0:most] = src[:, 0:most]

    def exchanged(ref, g, sem):
        rows = pl.ds(g * per_group * most, per_group * most)
        if g == 0:
            rows = (slice(None), pl.ds(most, (per_group - 1) * most))
        with jax.named_scope("wait"):
            pltpu.make_async_copy(ref.at[rows], ref.at[rows], sem.at[g]).wait()

    slots = lax.broadcasted_iota(I32, (gr, t_rows), 0)

    def gather(g):
        s0, s1 = (slots + g * gr == pos0), (slots + g * gr == pos1)
        chosen = (s0.astype(F32) + s1.astype(F32)).astype(BF16)
        rows = jnp.dot(chosen, tokens[...], preferred_element_type=F32)
        rows2d[...] = rows.astype(BF16)
        if g:
            to_tiles(rows2d, out3, g * gr)
        else:
            to_tiles(rows2d, fx.at[0], 0)

    sent = []

    def push(src, dst, send_sem, recv_sem, new_x):
        copy = pltpu.make_async_remote_copy(
            src_ref=src, dst_ref=dst, send_sem=send_sem, recv_sem=recv_sem,
            device_id=at_x(new_x), device_id_type=MESH,
        )
        copy.start()
        sent.append(copy)

    def arrive(ref, sem):
        with jax.named_scope("wait"):
            pltpu.make_async_copy(ref, ref, sem).wait()

    def rows_of(slot):
        return pl.ds(slot * gr, gr)

    def onward(way):
        (g,) = far
        rows = pl.ds(g * per_group * most, far_offsets * nc * most)
        dst, recv_sem = ((recv3, a2a_recv), (back3, back_recv))[way]
        arrive(relayed.at[way], relay_recv.at[way])
        copy = pltpu.make_async_remote_copy(
            src_ref=relayed.at[way], dst_ref=dst.at[rows], send_sem=relay_send.at[way], recv_sem=recv_sem.at[g],
            device_id=relative(1, -(nz // 4), 0, 0), device_id_type=MESH,
        )
        copy.start()
        sent.append(copy)

    def s1(g):
        exchanged(recv3, g, a2a_recv)
        from_tiles(block_in(recv3, g * gr), a2d.at[g])
        me = rows_of(0)
        push(a2d.at[g, me, lo], a2d.at[g, rows_of(1), lo], ag_send.at[g, 0], ag_recv.at[g, 0], right)
        push(a2d.at[g, me, hi], a2d.at[g, rows_of(2), hi], ag_send.at[g, 1], ag_recv.at[g, 1], left)
        push(a2d.at[g, me, hi], a2d.at[g, rows_of(1), hi], ag_send.at[g, 2], ag_recv.at[g, 2], right)
        push(a2d.at[g, me, lo], a2d.at[g, rows_of(2), lo], ag_send.at[g, 3], ag_recv.at[g, 3], left)

    def s2(g):
        arrive(a2d.at[g, rows_of(1), lo], ag_recv.at[g, 0])
        push(a2d.at[g, rows_of(1), lo], a2d.at[g, rows_of(3), lo], ag_send.at[g, 4], ag_recv.at[g, 4], right)
        arrive(a2d.at[g, rows_of(2), hi], ag_recv.at[g, 1])
        push(a2d.at[g, rows_of(2), hi], a2d.at[g, rows_of(3), hi], ag_send.at[g, 5], ag_recv.at[g, 5], left)

    def expert_hidden(g):
        while loads:
            loads.pop().wait()
        rows = a2d[g]
        by_unit = (((1,), (1,)), ((), ()))
        gate = lax.dot_general(rows, wg[...], by_unit, preferred_element_type=F32)
        up = lax.dot_general(rows, wu[...], by_unit, preferred_element_type=F32)
        hid[...] = (gate / (1.0 + jnp.exp(-gate)) * up).astype(BF16)

    def s3(g):
        arrive(a2d.at[g, rows_of(1), hi], ag_recv.at[g, 2])
        arrive(a2d.at[g, rows_of(2), lo], ag_recv.at[g, 3])
        arrive(a2d.at[g, rows_of(3), lo], ag_recv.at[g, 4])
        arrive(a2d.at[g, rows_of(3), hi], ag_recv.at[g, 5])
        expert_hidden(g)
        n_cols = half // 2
        for n in range(4):
            cols = slice(n * n_cols, (n + 1) * n_cols)
            res = jnp.dot(hid[...], wd[:, cols], preferred_element_type=F32)
            own[g, :, cols] = res[0:gr]
            to_left, to_right = res[gr : 2 * gr], res[2 * gr : 3 * gr]
            in_half = slice((n % 2) * n_cols, (n % 2 + 1) * n_cols)
            if n < 2:
                part[g, 0, :, cols] = to_left.astype(BF16)
                pf[g, 1, :, in_half] = to_right
            else:
                pf[g, 0, :, in_half] = to_left
                part[g, 1, :, cols] = to_right.astype(BF16)
            part[g, 2, :, cols] = res[3 * gr : 4 * gr].astype(BF16)
        push(part.at[g, 2, :, lo], rs1.at[g, 0], rs_send.at[g, 0], rs_recv.at[g, 0], right)
        push(part.at[g, 2, :, hi], rs1.at[g, 1], rs_send.at[g, 1], rs_recv.at[g, 1], left)
        push(part.at[g, 1, :, hi], rs2.at[g, 0, :, hi], rs_send.at[g, 2], rs_recv.at[g, 2], right)
        push(part.at[g, 0, :, lo], rs2.at[g, 1, :, lo], rs_send.at[g, 3], rs_recv.at[g, 3], left)

    def s4(g):
        arrive(rs1.at[g, 0], rs_recv.at[g, 0])
        part[g, 1, :, 0:half] = (pf[g, 1] + rs1[g, 0].astype(F32)).astype(BF16)
        push(part.at[g, 1, :, lo], rs2.at[g, 0, :, lo], rs_send.at[g, 4], rs_recv.at[g, 4], right)
        arrive(rs1.at[g, 1], rs_recv.at[g, 1])
        part[g, 0, :, half:width] = (pf[g, 0] + rs1[g, 1].astype(F32)).astype(BF16)
        push(part.at[g, 0, :, hi], rs2.at[g, 1, :, hi], rs_send.at[g, 5], rs_recv.at[g, 5], left)

    def s5(g):
        arrive(rs2.at[g, 0, :, hi], rs_recv.at[g, 2])
        arrive(rs2.at[g, 1, :, lo], rs_recv.at[g, 3])
        arrive(rs2.at[g, 0, :, lo], rs_recv.at[g, 4])
        arrive(rs2.at[g, 1, :, hi], rs_recv.at[g, 5])
        total = own[g] + rs2[g, 0].astype(F32) + rs2[g, 1].astype(F32)
        rows2d[...] = total.astype(BF16)
        to_tiles(rows2d, ret3, g * gr)
        exchange(ret3, back3, g, -1, back_send, back_recv)

    def s6(g):
        exchanged(back3, g, back_recv)
        from_tiles(block_in(back3, g * gr), rows2d)
        combine(g)

    def combine(g):
        rows = rows2d[...]
        res = jnp.dot(whi[g], rows, preferred_element_type=F32)
        res = res + jnp.dot(wlo[g], rows, preferred_element_type=F32)
        acc[...] = acc[...] + res

    top, low = pl.ds(0, gr // 2), pl.ds(gr // 2, gr - gr // 2)

    def n1():
        push(fx.at[0, top], fx.at[1, top], fx_send.at[0], fx_recv.at[0], right)
        push(fx.at[0, low], fx.at[2, low], fx_send.at[1], fx_recv.at[1], left)
        push(fx.at[0, low], fx.at[1, low], fx_send.at[2], fx_recv.at[2], right)
        push(fx.at[0, top], fx.at[2, top], fx_send.at[3], fx_recv.at[3], left)

    def n2():
        arrive(fx.at[1, top], fx_recv.at[0])
        push(fx.at[1, top], fx.at[3, top], fx_send.at[4], fx_recv.at[4], right)
        arrive(fx.at[2, low], fx_recv.at[1])
        push(fx.at[2, low], fx.at[3, low], fx_send.at[5], fx_recv.at[5], left)

    def n3():
        arrive(fx.at[1, low], fx_recv.at[2])
        arrive(fx.at[2, top], fx_recv.at[3])
        arrive(fx.at[3, top], fx_recv.at[4])
        arrive(fx.at[3, low], fx_recv.at[5])
        exchange(fx, fr, 0, 1, a2a_send, a2a_recv)

    def n4():
        exchanged(fr, 0, a2a_recv)
        for k in range(nx):
            from_tiles(block_in(fr.at[k], 0), a2d.at[0, rows_of(k)])
        expert_hidden(0)
        n_cols = width // 4
        for n in range(4):
            cols = slice(n * n_cols, (n + 1) * n_cols)
            a2d[0, :, cols] = jnp.dot(hid[...], wd[:, cols], preferred_element_type=F32).astype(BF16)
        for k in range(nx):
            to_tiles(a2d.at[0, rows_of(k)], fs.at[k], 0)
        exchange(fs, fb, 0, -1, back_send, back_recv)

    def n5():
        exchanged(fb, 0, back_recv)
        push(fb.at[3, top], f1.at[0], fb_send.at[0], fb_recv.at[0], right)
        push(fb.at[3, low], f1.at[1], fb_send.at[1], fb_recv.at[1], left)
        push(fb.at[2, low], f2.at[0, low], fb_send.at[2], fb_recv.at[2], right)
        push(fb.at[1, top], f2.at[1, top], fb_send.at[3], fb_recv.at[3], left)

    def n6():
        arrive(f1.at[0], fb_recv.at[0])
        fsum[0] = (fb[2, top].astype(F32) + f1[0].astype(F32)).astype(BF16)
        push(fsum.at[0], f2.at[0, top], fb_send.at[4], fb_recv.at[4], right)
        arrive(f1.at[1], fb_recv.at[1])
        fsum[1] = (fb[1, low].astype(F32) + f1[1].astype(F32)).astype(BF16)
        push(fsum.at[1], f2.at[1, low], fb_send.at[5], fb_recv.at[5], left)

    def n7():
        arrive(f2.at[0, low], fb_recv.at[2])
        arrive(f2.at[1, top], fb_recv.at[3])
        arrive(f2.at[0, top], fb_recv.at[4])
        arrive(f2.at[1, low], fb_recv.at[5])

        def summed(r):
            rows = slice(r, r + ROW_TILE)
            both = f2[0, rows].astype(F32) + f2[1, rows].astype(F32)
            return (fb[0, rows].astype(F32) + both).astype(BF16)

        from_tiles(summed, rows2d)
        combine(0)

    def send_counts():
        def one(i, carry):
            pltpu.make_async_remote_copy(
                src_ref=cnt_mine, dst_ref=cnt_all.at[i], send_sem=cnt_send, recv_sem=cnt_recv,
                device_id=relative(1, *split(i)), device_id_type=MESH,
            ).start()
            return carry

        lax.fori_loop(1, plane, one, 0)

    counted = {}

    def plane_counts():
        arrive(cnt_all.at[pl.ds(1, plane - 1)], cnt_recv)
        table = cnt_all[:, 0, 0:n_experts]
        i = lax.broadcasted_iota(I32, (plane, 1), 0)
        sz = (z - lax.shift_right_logical(i, log2(per_z)) + nz) & (nz - 1)
        sy = (y - (lax.shift_right_logical(i, log2(nc)) & (ny - 1)) + ny) & (ny - 1)
        sc = (c - (i & (nc - 1)) + nc) & (nc - 1)
        mine = (z * ny + y) * nc + c
        first = ((sz * ny + sy) * nc + sc < mine).astype(F32)
        counted["inside"] = jnp.sum(table * first, axis=0, keepdims=True)
        tot_mine[:, 0:n_experts] = jnp.sum(table, axis=0, keepdims=True)
        for k, new_x in enumerate((right, left, opp)):
            push(tot_mine, tot_all.at[k], tot_send.at[k], tot_recv.at[k], new_x)

    def weigh():
        small[2].wait()
        small[3].wait()
        offset = counted["inside"]
        for k, src in enumerate((left, right, opp)):
            arrive(tot_all.at[k], tot_recv.at[k])
            offset = offset + tot_all[k][:, 0:n_experts] * jnp.where(src < x, 1.0, 0.0)
        diagonal = lax.broadcasted_iota(I32, (n_experts, n_experts), 0) == lax.broadcasted_iota(
            I32, (n_experts, n_experts), 1
        )

        def down(row):
            return jnp.sum(jnp.where(diagonal, row, 0.0), axis=1, keepdims=True)

        offset, limit = down(offset), down(cap[...].astype(F32))
        parts = []
        for k, (oh, rank, pos) in enumerate(((oh0, rank0, pos0), (oh1, rank1, pos1))):
            slot = jnp.sum(oh * offset, axis=0, keepdims=True) + rank
            top = jnp.sum(oh * limit, axis=0, keepdims=True)
            unit = jnp.where(slot < top, units[k : k + 1, :], 0)
            high = unit & ~7
            parts.append((pos, high.astype(F32) / 1024.0, (unit - high).astype(F32) / 1024.0))
        wide = lax.broadcasted_iota(I32, (LANES, t_rows), 0)
        for g in range(len(groups)):
            h = l = jnp.zeros((LANES, t_rows), F32)
            for pos, high, low in parts:
                here = wide + g * gr == pos
                h, l = h + jnp.where(here, high, 0.0), l + jnp.where(here, low, 0.0)
            whi[g] = jnp.transpose(h)[:, 0:gr].astype(BF16)
            wlo[g] = jnp.transpose(l)[:, 0:gr].astype(BF16)
        acc[...] = jnp.zeros_like(acc)

    n = len(groups)
    steps = nz // 2 - 1

    def dispatch(g):
        gather(g)
        exchange(out3, recv3, g, 1, a2a_send, a2a_recv)

    def enter():
        gather(0)
        with jax.named_scope("barrier"):
            near_ready()

    def relay(step):
        told(step)
        if step + 1 < steps:
            tell(step + 1)

    if n == 4:
        order = [
            (enter,), (n1,), (tell, 0), (relay, 0), (dispatch, 3), (relay, 1), (n2,), (relay, 2), (dispatch, 1),
            (s1, 3), (dispatch, 2), (s2, 3), (s1, 1), (send_counts,), (onward, 0), (s2, 1), (n3,), (s1, 2), (s3, 1),
            (s2, 2), (n4,), (s4, 1), (s3, 2), (s5, 1), (plane_counts,), (s4, 2), (s3, 3), (s5, 2), (s4, 3), (n5,),
            (weigh,), (onward, 1), (s5, 3), (s6, 1), (n6,), (n7,), (s6, 2), (s6, 3),
        ]
    else:
        order = [(enter,), (n1,), (tell, 0)] + [(relay, step) for step in range(steps)]
        order += [(dispatch, g) for g in range(1, n)] + [(n2,), (n3,), (onward, 0)]
        order += [(stage, g) for stage in (s1, s2, s3, s4, s5) for g in range(1, n)]
        order += [(n4,), (send_counts,), (plane_counts,), (weigh,), (n5,), (n6,), (onward, 1)] + [(s6, g) for g in range(1, n)] + [(n7,)]
    for stage, *args in order:
        with jax.named_scope("_".join([stage.__name__, *map(str, args)])):
            stage(*args)
    out[...] = acc[...].astype(BF16)

    for copy in sent:
        copy.wait_send()
    exchanged(fx, 0, a2a_send)
    exchanged(fs, 0, back_send)
    for g in range(1, n):
        exchanged(out3, g, a2a_send)
        exchanged(ret3, g, back_send)
    arrive(cnt_all.at[pl.ds(1, plane - 1)], cnt_send)


def local(shape, most, tokens, expert_ids, gate_units, capacity, w_gate, w_up, w_down):
    nx, nz, ny, nc = shape
    t_rows, width = tokens.shape
    ff = w_gate.shape[2]
    turn = functools.partial(jnp.swapaxes, axis1=-1, axis2=-2)
    plane = nz * ny * nc
    groups = offset_groups(nz, ny)
    n, gr = len(groups), len(groups[0]) * nc * most
    vmem = pl.BlockSpec(memory_space=pltpu.VMEM)
    in_hbm = pl.BlockSpec(memory_space=pltpu.HBM)
    stay = functools.partial(pltpu.with_memory_space_constraint, memory_space=pltpu.HBM)
    dma = pltpu.SemaphoreType.DMA
    near_tiles = pltpu.VMEM((nx, gr, ROW_TILE, LANES), BF16)
    tiles = pltpu.VMEM((plane * most, ROW_TILE, LANES), BF16)
    return pl.pallas_call(
        functools.partial(kernel, shape, most),
        out_shape=jax.ShapeDtypeStruct((t_rows, width), BF16),
        in_specs=[in_hbm] * 7,
        out_specs=vmem,
        scratch_shapes=[
            pltpu.VMEM((t_rows, width), BF16),
            pltpu.VMEM((2, t_rows), I32),
            pltpu.VMEM((2, t_rows), I32),
            pltpu.VMEM((1, plane), I32),
            pltpu.VMEM((ff, width), BF16),
            pltpu.VMEM((ff, width), BF16),
            pltpu.VMEM((ff, width), BF16),
            pltpu.VMEM((256, 256), BF16),
            pltpu.VMEM((gr, width), BF16),
            tiles, tiles, tiles, tiles,
            pltpu.VMEM((n, nx * gr, width), BF16),
            pltpu.VMEM((nx * gr, ff), BF16),
            pltpu.VMEM((n, gr, width), F32),
            pltpu.VMEM((n, 2, gr, width // 2), F32),
            pltpu.VMEM((n, 3, gr, width), BF16),
            pltpu.VMEM((n, 2, gr, width // 2), BF16),
            pltpu.VMEM((n, 2, gr, width), BF16),
            pltpu.VMEM((8, LANES), F32),
            pltpu.VMEM((n, t_rows, gr), BF16),
            pltpu.VMEM((n, t_rows, gr), BF16),
            pltpu.VMEM((t_rows, width), F32),
            pltpu.VMEM((1, LANES), F32),
            pltpu.VMEM((plane, 1, LANES), F32),
            pltpu.VMEM((1, LANES), F32),
            pltpu.VMEM((3, 1, LANES), F32),
            near_tiles, near_tiles, near_tiles, near_tiles,
            pltpu.VMEM((2, gr // 2, ROW_TILE, LANES), BF16),
            pltpu.VMEM((2, gr, ROW_TILE, LANES), BF16),
            pltpu.VMEM((2, gr // 2, ROW_TILE, LANES), BF16),
            pltpu.VMEM((2, min(2, ny) * nc * most, ROW_TILE, LANES), BF16),
            pltpu.SemaphoreType.REGULAR((nz // 2 - 1,)),
            dma((7,)),
            dma((n,)), dma((n,)),
            dma((n, 6)), dma((n, 6)),
            dma((n, 6)), dma((n, 6)),
            dma((n,)), dma((n,)),
            dma, dma,
            dma((3,)), dma((3,)),
            dma((6,)), dma((6,)),
            dma((6,)), dma((6,)),
            dma((2,)), dma((2,)),
        ],
        compiler_params=pltpu.CompilerParams(collective_id=0, has_side_effects=True, vmem_limit_bytes=56000000),
    )(
        tokens, stay(turn(expert_ids)), stay(turn(gate_units)), stay(capacity.reshape(1, -1)),
        turn(w_gate), turn(w_up), turn(w_down),
    )


def build(finer, most):
    shape = tuple(finer.shape[a] for a in AXES)
    return jax.shard_map(
        functools.partial(local, shape, most),
        mesh=finer,
        in_specs=(
            P(AXES, None),
            P(AXES, None),
            P(AXES, None),
            P(),
            P(EXPERT, None, "dp"),
            P(EXPERT, None, "dp"),
            P(EXPERT, None, "dp"),
        ),
        out_specs=P(AXES, None),
        check_vma=False,
    )


def solution(mesh):
    finer = Mesh(mesh.devices.reshape(mesh.shape["dp"], 8, 4, 2), AXES)
    return build(finer, 5)
```

profile of v0, /device:TPU:1, one launch (start us, length us, event | category | flops | bytes accessed | tf_op | source)
XLA Modules:
  0.0 105.6 jit_solution(1453222912203394902)
XLA Ops:
  0.0 104.8 %shard_map.73 = bf16[128,2048]{1,0:T(8,128)(2,1)S(1)} custom-call(bf16[128,2048]{1,0:T(8,128)(2,1)} %tokens_h.1, s32[2,128]{1,0:T(2,128)} %bitcast.9, s32[2,128]{1,0:T(2,128)} %bitcast.10, s32[1,64]{1,0:T(1,128)} %bitcast.11, bf16[1,352,2048]{2,1,0:T(8,128)(2,1)} %bitcast.6, bf16[1,352,2048]{2,1,0:T(8,128)(2,1)} %bitcast.7, bf16[1,352,2048]{2,1,0:T(8,128)(2,1)} %bitcast.8), custom_call_target="tpu_custom_call" | custom-call | tf_op jit(solution)/shard_map/pallas_call | solution.py:500
  104.8 0.8 copy.9
where the time goes:
time: 106 us
  Pallas kernels  105 us (99%)
    pallas_call x1, Pallas kernels, local(): pl.pallas_call(functools.partial(kernel, shape, most), out_shape=jax.Shap...  105 us

commit v1 on v0

--- a/solution.py
+++ b/solution.py
@@ -24,8 +24,8 @@
         ]
     return [
         [(0, 0), (0, 1), (0, 2), (0, 3), (1, 0), (-1, 0), (1, 3), (-1, 3)],
-        [(-2, 2), (-2, 3), (2, 2), (2, 3), (3, 0), (-3, 0), (3, 1), (-3, 1)],
-        [(4, 0), (4, 1), (3, 2), (3, 3), (-3, 2), (-3, 3), (4, 2), (4, 3)],
+        [(-2, 2), (2, 2), (3, 0), (-3, 0), (3, 1), (-3, 1), (3, 2), (-3, 2)],
+        [(4, 0), (4, 1), (-2, 3), (2, 3), (3, 3), (-3, 3), (4, 2), (4, 3)],
         [(1, 1), (-1, 1), (1, 2), (-1, 2), (2, 0), (-2, 0), (2, 1), (-2, 1)],
     ]
 
@@ -312,11 +312,19 @@
         from_tiles(block_in(back3, g * gr), rows2d)
         combine(g)
 
+    combined = []
+
     def combine(g):
         rows = rows2d[...]
         res = jnp.dot(whi[g], rows, preferred_element_type=F32)
         res = res + jnp.dot(wlo[g], rows, preferred_element_type=F32)
-        acc[...] = acc[...] + res
+        combined.append(g)
+        if len(combined) == len(groups):
+            out[...] = (acc[...] + res).astype(BF16)
+        elif len(combined) == 1:
+            acc[...] = res
+        else:
+            acc[...] = acc[...] + res
 
     top, low = pl.ds(0, gr // 2), pl.ds(gr // 2, gr - gr // 2)
 
@@ -437,7 +445,6 @@
                 h, l = h + jnp.where(here, high, 0.0), l + jnp.where(here, low, 0.0)
             whi[g] = jnp.transpose(h)[:, 0:gr].astype(BF16)
             wlo[g] = jnp.transpose(l)[:, 0:gr].astype(BF16)
-        acc[...] = jnp.zeros_like(acc)
 
     n = len(groups)
     steps = nz // 2 - 1
@@ -471,7 +478,6 @@
     for stage, *args in order:
         with jax.named_scope("_".join([stage.__name__, *map(str, args)])):
             stage(*args)
-    out[...] = acc[...].astype(BF16)
 
     for copy in sent:
         copy.wait_send()

time: 106 us -> 105 us (level)
  no operation moved by 1% of the time
where the time goes in v1:
time: 105 us
  Pallas kernels  104 us (99%)
    pallas_call x1, Pallas kernels, local(): pl.pallas_call(functools.partial(kernel, shape, most), out_shape=jax.Shap...  104 us

profile of v1, /device:TPU:1, one launch (start us, length us, event | category | flops | bytes accessed | tf_op | source)
XLA Modules:
  0.0 105.2 jit_solution(13968869723203674129)
XLA Ops:
  0.0 104.4 %shard_map.73 = bf16[128,2048]{1,0:T(8,128)(2,1)S(1)} custom-call(bf16[128,2048]{1,0:T(8,128)(2,1)} %tokens_h.1, s32[2,128]{1,0:T(2,128)} %bitcast.9, s32[2,128]{1,0:T(2,128)} %bitcast.10, s32[1,64]{1,0:T(1,128)} %bitcast.11, bf16[1,352,2048]{2,1,0:T(8,128)(2,1)} %bitcast.6, bf16[1,352,2048]{2,1,0:T(8,128)(2,1)} %bitcast.7, bf16[1,352,2048]{2,1,0:T(8,128)(2,1)} %bitcast.8), custom_call_target="tpu_custom_call" | custom-call | tf_op jit(solution)/shard_map/pallas_call | solution.py:506
  104.4 0.8 copy.9

commit v2 on v1

--- a/solution.py
+++ b/solution.py
@@ -467,8 +467,8 @@
         order = [
             (enter,), (n1,), (tell, 0), (relay, 0), (dispatch, 3), (relay, 1), (n2,), (relay, 2), (dispatch, 1),
             (s1, 3), (dispatch, 2), (s2, 3), (s1, 1), (send_counts,), (onward, 0), (s2, 1), (n3,), (s1, 2), (s3, 1),
-            (s2, 2), (n4,), (s4, 1), (s3, 2), (s5, 1), (plane_counts,), (s4, 2), (s3, 3), (s5, 2), (s4, 3), (n5,),
-            (weigh,), (onward, 1), (s5, 3), (s6, 1), (n6,), (n7,), (s6, 2), (s6, 3),
+            (s2, 2), (s4, 1), (n4,), (s3, 2), (s5, 1), (plane_counts,), (s4, 2), (s3, 3), (s5, 2), (s4, 3), (n5,),
+            (weigh,), (onward, 1), (s5, 3), (s6, 1), (n6,), (s6, 2), (n7,), (s6, 3),
         ]
     else:
         order = [(enter,), (n1,), (tell, 0)] + [(relay, step) for step in range(steps)]

time: 105 us -> 106 us (level); the launches traced: 105 us -> 105 us
  no operation moved by 1% of the time
where the time goes in v2:
time: 106 us; the launch traced here: 105 us
  Pallas kernels  104 us (98%)
    pallas_call x1, Pallas kernels, local(): pl.pallas_call(functools.partial(kernel, shape, most), out_shape=jax.Shap...  104 us

profile of v2, /device:TPU:1, one launch (start us, length us, event | category | flops | bytes accessed | tf_op | source)
XLA Modules:
  0.0 104.6 jit_solution(2953525593026108239)
XLA Ops:
  0.0 103.8 %shard_map.73 = bf16[128,2048]{1,0:T(8,128)(2,1)S(1)} custom-call(bf16[128,2048]{1,0:T(8,128)(2,1)} %tokens_h.1, s32[2,128]{1,0:T(2,128)} %bitcast.9, s32[2,128]{1,0:T(2,128)} %bitcast.10, s32[1,64]{1,0:T(1,128)} %bitcast.11, bf16[1,352,2048]{2,1,0:T(8,128)(2,1)} %bitcast.6, bf16[1,352,2048]{2,1,0:T(8,128)(2,1)} %bitcast.7, bf16[1,352,2048]{2,1,0:T(8,128)(2,1)} %bitcast.8), custom_call_target="tpu_custom_call" | custom-call | tf_op jit(solution)/shard_map/pallas_call | solution.py:506
  103.9 0.8 copy.9
